TPU v7x, 32 devices: a whole 2x2x4 slice. The times are simulated.
32 devices in a mesh: row: 4 (over x, core), col: 8 (over z, y).
Axes of the slice: x: 2, y: 2, z: 4, core: 2. Of those that a mesh axis runs over, the one named last changes fastest.
Arguments:
- jump: float32 [3, 256, 1024], P(None, 'row', 'col'), may hold values from -6 to 6
- external: float32 [3, 256, 1024], P(None, 'row', 'col'), may hold values from -12 to 12
- cohesive: float32 [256, 1024], P('row', 'col'), may hold values from 0.5 to 4
- bond_mask: int32 [2, 256, 1024], P(None, 'row', 'col'), may hold values 0 or 1
- load_factor: float32 [1], replicated, may hold values from 0.5 to 1.5
- arc_radius: float32 [1], replicated, may hold values from 0.5 to 1.5
- stiffness: bfloat16 [1536, 1536], replicated, may hold values from -1 to 2
- coupling: float32 [3, 1536], replicated, may hold values from -6 to 6
- old_state: float32 [5120, 1536], P(('row', 'col')), may hold values from -3 to 3
- old_history: float32 [5120, 1536], P(('row', 'col')), may hold values from 0 to 1.5
- newton_steps: int32 [5120], P(('row', 'col')), may hold values from 0 to 9, as said below
- point_ids: int32 [5120], P(('row', 'col')), may hold values from 0 to 8191, as said below
Outputs:
- new_jump: float32 [3, 256, 1024], P(None, 'row', 'col')
- new_load: float32 [1], replicated
- new_state: float32 [2560, 1536], P(('row', 'col'))
- new_history: float32 [2560, 1536], P(('row', 'col'))
Inputs may be any that keep to these rules, and one draw needn't show every extreme that they name: `newton_steps`: within one block the live slots number between 20 and 160, and some block has all 160 live; in all at most 2240 slots are live; a live slot's count is at least 2. `point_ids`: the slots of one block name distinct points of that block.
All inputs are finite; a program needn't handle non-finite values. No bound on the sum of `bond_mask` on one device may be relied on, other than what follows from the above.
Results may differ from a plain program's by a relative error of at most 0.0028.
Values sent between devices are 32-bit elements; how exact they have to be, the bound alone decides.
A program may use at most 64 MiB of HBM per device.

v0:
```python
import jax
import jax.numpy as jnp
from jax import lax
from jax.sharding import PartitionSpec as P

MAX_STEPS = 9
SWEEPS = 3


softening = 1.0


def shifted_2(value, axis, steps):
    count = lax.axis_size(axis)
    first, last = (max(0, -steps), min(count, count - steps))
    return lax.ppermute(value, axis, [(source, source + steps) for source in range(first, last)])


def extended(cells, sides, width):
    for axis, dim in sides:
        count = lax.axis_size(axis)
        ends = count - 1
        head = lax.slice_in_dim(cells, 0, width, axis=dim)
        tail = lax.slice_in_dim(cells, cells.shape[dim] - width, cells.shape[dim], axis=dim)
        cells = jnp.concatenate(
            [
                lax.ppermute(tail, axis, [(i, (i + 1) % count) for i in range(ends)]),
                cells,
                lax.ppermute(head, axis, [((i + 1) % count, i) for i in range(ends)]),
            ],
            axis=dim,
        )
    return cells


def micro_solve(state, history, drive, steps, stiffness, coupling):
    diagonal = jnp.diagonal(stiffness).astype(jnp.float32)
    load = jnp.dot(drive, coupling, precision=lax.Precision.HIGHEST)
    damage = jnp.exp(-history)

    def advance(count, current):
        bent = jnp.tanh(current)
        force = jnp.dot(current.astype(jnp.bfloat16), stiffness, preferred_element_type=jnp.float32)
        misfit = force + softening * damage * bent - load
        slope = diagonal + softening * damage * (1.0 - bent * bent)
        return jnp.where((count < steps)[:, None], current - misfit / slope, current)

    state = lax.fori_loop(0, MAX_STEPS, advance, state)
    bent = jnp.tanh(state)
    cells = state.shape[1]
    traction = (
        jnp.dot(softening * damage * bent, coupling.T, precision=lax.Precision.HIGHEST) / cells
    )
    weight = softening * damage * (1.0 - bent * bent)
    products = jnp.stack(
        [
            coupling[0] * coupling[0],
            coupling[1] * coupling[1],
            coupling[2] * coupling[2],
            coupling[0] * coupling[1],
            coupling[0] * coupling[2],
            coupling[1] * coupling[2],
        ]
    )
    tangent = jnp.dot(weight, products.T, precision=lax.Precision.HIGHEST) / cells
    history = jnp.maximum(history, jnp.abs(state))
    return (state, history, traction, tangent)


def block_solve(scale, tangent, source):
    d00 = scale + tangent[0]
    d11 = scale + tangent[1]
    d22 = scale + tangent[2]
    d01, d02, d12 = (tangent[3], tangent[4], tangent[5])
    c00 = d11 * d22 - d12 * d12
    c11 = d00 * d22 - d02 * d02
    c22 = d00 * d11 - d01 * d01
    c01 = d02 * d12 - d01 * d22
    c02 = d01 * d12 - d02 * d11
    c12 = d01 * d02 - d00 * d12
    determinant = d00 * c00 + d01 * c01 + d02 * c02
    first = (c00 * source[0] + c01 * source[1] + c02 * source[2]) / determinant
    second = (c01 * source[0] + c11 * source[1] + c12 * source[2]) / determinant
    third = (c02 * source[0] + c12 * source[1] + c22 * source[2]) / determinant
    return jnp.stack([first, second, third])


def neighbours(padded, bond_x, low_x, bond_y, low_y):
    return (
        bond_x * padded[:, 2:, 1:-1]
        + low_x * padded[:, :-2, 1:-1]
        + bond_y * padded[:, 1:-1, 2:]
        + low_y * padded[:, 1:-1, :-2]
    )


def on_device(
    jump,
    external,
    cohesive,
    bond_mask,
    load_factor,
    arc_radius,
    stiffness,
    coupling,
    old_state,
    old_history,
    newton_steps,
    point_ids,
):
    devices = lax.axis_size(("row", "col"))
    here = lax.axis_index(("row", "col"))
    slots, cells = old_state.shape
    new_cap = slots // 2
    pair = 2 * ((slots + 2 * devices + 1) // (2 * devices))
    width = devices * pair
    rows_x, rows_y = (jump.shape[1], jump.shape[2])
    live = newton_steps > 0
    live_int = live.astype(jnp.int32)
    live_float = live.astype(jnp.float32)
    counts = lax.all_gather(jnp.sum(live_int)[None], ("row", "col"), axis=0, tiled=True)
    starts = jnp.cumsum(counts, dtype=jnp.int32) - counts
    rank = starts[here] + jnp.cumsum(live_int, dtype=jnp.int32) - live_int
    home_block = rank // 2 % devices
    peers = jnp.arange(devices, dtype=jnp.int32)
    aimed = ((home_block[:, None] == peers[None, :]) & live[:, None]).astype(jnp.int32)
    within = jnp.sum((jnp.cumsum(aimed, axis=0, dtype=jnp.int32) - aimed) * aimed, axis=1)
    send_index = jnp.where(live, home_block * pair + within, width)
    new_slot = jnp.arange(new_cap, dtype=jnp.int32)
    wanted = 2 * (here + devices * (new_slot // 2)) + new_slot % 2
    valid = wanted < jnp.sum(counts)
    source = jnp.sum((starts[None, :] <= wanted[:, None]).astype(jnp.int32), axis=1) - 1
    coming = ((source[:, None] == peers[None, :]) & valid[:, None]).astype(jnp.int32)
    order = jnp.sum((jnp.cumsum(coming, axis=0, dtype=jnp.int32) - coming) * coming, axis=1)
    recv_index = jnp.where(valid, source * pair + order, 0)
    drive = jump.reshape(3, rows_x * rows_y)[:, point_ids].T
    blank = jnp.zeros((width, cells), jnp.float32)
    state, history, traction, tangent = micro_solve(
        old_state, old_history, drive, newton_steps, stiffness, coupling
    )
    outgoing = (
        blank.at[send_index].set(state, mode="drop"),
        blank.at[send_index].set(history, mode="drop"),
    )
    arrived = (
        lax.all_to_all(outgoing[0], ("row", "col"), split_axis=0, concat_axis=0, tiled=True),
        lax.all_to_all(outgoing[1], ("row", "col"), split_axis=0, concat_axis=0, tiled=True),
    )
    new_state = jnp.where(valid[:, None], arrived[0][recv_index], 0.0)
    new_history = jnp.where(valid[:, None], arrived[1][recv_index], 0.0)
    points = rows_x * rows_y
    soft = jnp.zeros((points,), jnp.float32).at[point_ids].add(live_float).reshape(rows_x, rows_y)
    rve_traction = (
        jnp.zeros((3, points), jnp.float32)
        .at[:, point_ids]
        .add((traction * live_float[:, None]).T)
        .reshape(3, rows_x, rows_y)
    )
    rve_tangent = (
        jnp.zeros((6, points), jnp.float32)
        .at[:, point_ids]
        .add((tangent * live_float[:, None]).T)
        .reshape(6, rows_x, rows_y)
    )
    bond_x = 0.25 + 0.75 * bond_mask[0].astype(jnp.float32)
    bond_y = 0.25 + 0.75 * bond_mask[1].astype(jnp.float32)
    edge_x = shifted_2(bond_x[-1:, :], "row", 1)
    edge_y = shifted_2(bond_y[:, -1:], "col", 1)
    low_x = jnp.concatenate([edge_x, bond_x[:-1]], axis=0)
    low_y = jnp.concatenate([edge_y, bond_y[:, :-1]], axis=1)
    scale = bond_x + low_x + bond_y + low_y + (1.0 - soft) * cohesive
    padded_jump = extended(jump, (("row", 1), ("col", 2)), 1)
    residual = (
        scale * jump
        - neighbours(padded_jump, bond_x, low_x, bond_y, low_y)
        + rve_traction
        - load_factor[0] * external
    )
    source_terms = jnp.concatenate([-residual, external])

    def solve_both(values):
        return jnp.concatenate(
            [
                block_solve(scale, rve_tangent, values[:3]),
                block_solve(scale, rve_tangent, values[3:]),
            ]
        )

    iterate = solve_both(source_terms)
    for sweep in range(SWEEPS):
        padded = extended(iterate, (("row", 1), ("col", 2)), 1)
        iterate = solve_both(source_terms + neighbours(padded, bond_x, low_x, bond_y, low_y))
    correction, direction = (iterate[:3], iterate[3:])
    cross, square = lax.psum(
        (jnp.sum(correction * direction), jnp.sum(direction * direction)), ("row", "col")
    )
    entries = 3.0 * rows_x * rows_y * devices
    shifted = square + 0.25 * entries
    increment = (arc_radius[0] * jnp.sqrt(entries) * jnp.sqrt(shifted) - cross) / shifted
    new_jump = jump + correction + increment * direction
    new_load = load_factor + increment
    return (new_jump, new_load, new_state, new_history)


def solution(mesh):
    in_specs = (
        P(None, "row", "col"),
        P(None, "row", "col"),
        P("row", "col"),
        P(None, "row", "col"),
        P(),
        P(),
        P(),
        P(),
        P(("row", "col"), None),
        P(("row", "col"), None),
        P(("row", "col")),
        P(("row", "col")),
    )
    out_specs = (P(None, "row", "col"), P(), P(("row", "col"), None), P(("row", "col"), None))
    return jax.shard_map(
        on_device, mesh=mesh, in_specs=in_specs, out_specs=out_specs, check_vma=False
    )
```

profile of v0, /device:TPU:0, one launch (start us, length us, event | category | flops | bytes accessed | tf_op | source)
XLA Modules:
  0.0 336.0 jit_solution(9849236798043619368)
XLA Ops:
  0.7 1.4 fusion.110
  3.3 3.6 %collective-permute-start.3 = (f32[3,1,128]{2,1,0:T(1,128)}, f32[3,1,128]{2,1,0:T(1,128)}, u32[]{:S(2)}, u32[]{:S(2)}) collective-permute-start(f32[3,1,128]{2,1,0:T(1,128)} %get-tuple-element.191), channel_id=1, source_target_pairs={{0,8},{8,16},{16,24},{1,9},{9,17},{17,25},{2,10},{10,18},{18,26},{... | collective-permute-start | bytes 4616 | tf_op jit(solution)/shard_map/ppermute | solution.py:27
  7.0 1.4 fusion.95
  8.9 4.5 %collective-permute-start = (f32[1,128]{1,0:T(1,128)}, f32[1,128]{1,0:T(1,128)}, u32[]{:S(2)}, u32[]{:S(2)}) collective-permute-start(f32[1,128]{1,0:T(1,128)} %slice_bitcast_fusion.22), channel_id=1, source_target_pairs={{0,8},{8,16},{16,24},{1,9},{9,17},{17,25},{2,10},{10,18},{18,26},{... | collective-permute-start | bytes 1544 | tf_op jit(solution)/shard_map/ppermute | solution.py:16
  14.0 4.0 %collective-permute-start.1 = (f32[64,1]{1,0:T(8,128)}, f32[64,1]{1,0:T(8,128)}, u32[]{:S(2)}, u32[]{:S(2)}) collective-permute-start(f32[64,1]{1,0:T(8,128)} %slice.472), channel_id=1, source_target_pairs={{0,1},{1,2},{2,3},{3,4},{4,5},{5,6},{6,7},{8,9},{9,10},{10,11},{11... | collective-permute-start | bytes 776 | tf_op jit(solution)/shard_map/ppermute | solution.py:16
  18.1 3.4 %copy.28 = f32[3,64,128]{0,2,1:T(8,128)} copy(f32[3,64,128]{2,1,0:T(8,128)} %param.14) | data formatting | bytes 196608 | tf_op args[0]
  22.1 24.3 %gather_fusion.1 = bf16[1536]{0:T(1024)(128)(2,1)S(1)} fusion(bf16[1536,1536]{1,0:T(8,128)(2,1)} %param.20, s32[1536]{0:T(1024)S(1)} %or_reduce_fusion), kind=kCustom, calls=%fused_computation.1 | custom fusion | bytes 18432 | tf_op jit(solution)/shard_map/jit(diagonal)/cond/branch_0_fun/gather | solution.py:37
  47.0 2.9 gather_fusion
  49.9 1.9 fusion.113
  51.8 34.3 %while.13 = (s32[]{:T(128)}, f32[160,1536]{1,0:T(8,128)S(1)}, s32[160]{0:T(256)S(1)}, bf16[1536,1536]{1,0:T(8,128)(2,1)}, f32[160,1536]{1,0:T(8,128)S(1)}, /*ind...) while((s32[]{:T(128)}, f32[160,1536]{1,0:T(8,128)S(1)}, s32[160]{0:T(256)S(1)}, ...), condition=%wide.region_2.3_spmd, body=%wide.region_1.0_spmd.sunk | while | flops 757678272 | bytes 10624033 | solution.py:48
  51.8 3.7 %fusion.124 = f32[160,1536]{1,0:T(8,128)S(1)} fusion(f32[160,1536]{1,0:T(8,128)S(1)} %copy.66, f32[160,1536]{1,0:T(8,128)} %get-tuple-element.272, bf16[1536,1536]{1,0:T(8,128)(2,1)} %get-tuple-element.270, f32[160,1536]{1,0:T(8,128)S(1)} %get-tuple-element.271, f32[1536]{0:T(1024)S(1)} %get-tuple-element.273, ...), kind=kOutput, calls=%fused_computation.13.clone.1 | convolution fusion | flops 757678080 | bytes 8657056 | tf_op jit(solution)/shard_map/while/body/eval_jaxpr/dot_general | solution.py:43
  55.7 3.7 %fusion.124 = f32[160,1536]{1,0:T(8,128)S(1)} fusion(f32[160,1536]{1,0:T(8,128)S(1)} %copy.66, f32[160,1536]{1,0:T(8,128)} %get-tuple-element.272, bf16[1536,1536]{1,0:T(8,128)(2,1)} %get-tuple-element.270, f32[160,1536]{1,0:T(8,128)S(1)} %get-tuple-element.271, f32[1536]{0:T(1024)S(1)} %get-tuple-element.273, ...), kind=kOutput, calls=%fused_computation.13.clone.1 | convolution fusion | flops 757678080 | bytes 8657056 | tf_op jit(solution)/shard_map/while/body/eval_jaxpr/dot_general | solution.py:43
  59.5 3.7 %fusion.124 = f32[160,1536]{1,0:T(8,128)S(1)} fusion(f32[160,1536]{1,0:T(8,128)S(1)} %copy.66, f32[160,1536]{1,0:T(8,128)} %get-tuple-element.272, bf16[1536,1536]{1,0:T(8,128)(2,1)} %get-tuple-element.270, f32[160,1536]{1,0:T(8,128)S(1)} %get-tuple-element.271, f32[1536]{0:T(1024)S(1)} %get-tuple-element.273, ...), kind=kOutput, calls=%fused_computation.13.clone.1 | convolution fusion | flops 757678080 | bytes 8657056 | tf_op jit(solution)/shard_map/while/body/eval_jaxpr/dot_general | solution.py:43
  63.3 3.7 %fusion.124 = f32[160,1536]{1,0:T(8,128)S(1)} fusion(f32[160,1536]{1,0:T(8,128)S(1)} %copy.66, f32[160,1536]{1,0:T(8,128)} %get-tuple-element.272, bf16[1536,1536]{1,0:T(8,128)(2,1)} %get-tuple-element.270, f32[160,1536]{1,0:T(8,128)S(1)} %get-tuple-element.271, f32[1536]{0:T(1024)S(1)} %get-tuple-element.273, ...), kind=kOutput, calls=%fused_computation.13.clone.1 | convolution fusion | flops 757678080 | bytes 8657056 | tf_op jit(solution)/shard_map/while/body/eval_jaxpr/dot_general | solution.py:43
  67.1 3.7 %fusion.124 = f32[160,1536]{1,0:T(8,128)S(1)} fusion(f32[160,1536]{1,0:T(8,128)S(1)} %copy.66, f32[160,1536]{1,0:T(8,128)} %get-tuple-element.272, bf16[1536,1536]{1,0:T(8,128)(2,1)} %get-tuple-element.270, f32[160,1536]{1,0:T(8,128)S(1)} %get-tuple-element.271, f32[1536]{0:T(1024)S(1)} %get-tuple-element.273, ...), kind=kOutput, calls=%fused_computation.13.clone.1 | convolution fusion | flops 757678080 | bytes 8657056 | tf_op jit(solution)/shard_map/while/body/eval_jaxpr/dot_general | solution.py:43
  70.9 3.7 %fusion.124 = f32[160,1536]{1,0:T(8,128)S(1)} fusion(f32[160,1536]{1,0:T(8,128)S(1)} %copy.66, f32[160,1536]{1,0:T(8,128)} %get-tuple-element.272, bf16[1536,1536]{1,0:T(8,128)(2,1)} %get-tuple-element.270, f32[160,1536]{1,0:T(8,128)S(1)} %get-tuple-element.271, f32[1536]{0:T(1024)S(1)} %get-tuple-element.273, ...), kind=kOutput, calls=%fused_computation.13.clone.1 | convolution fusion | flops 757678080 | bytes 8657056 | tf_op jit(solution)/shard_map/while/body/eval_jaxpr/dot_general | solution.py:43
  74.7 3.7 %fusion.124 = f32[160,1536]{1,0:T(8,128)S(1)} fusion(f32[160,1536]{1,0:T(8,128)S(1)} %copy.66, f32[160,1536]{1,0:T(8,128)} %get-tuple-element.272, bf16[1536,1536]{1,0:T(8,128)(2,1)} %get-tuple-element.270, f32[160,1536]{1,0:T(8,128)S(1)} %get-tuple-element.271, f32[1536]{0:T(1024)S(1)} %get-tuple-element.273, ...), kind=kOutput, calls=%fused_computation.13.clone.1 | convolution fusion | flops 757678080 | bytes 8657056 | tf_op jit(solution)/shard_map/while/body/eval_jaxpr/dot_general | solution.py:43
  78.5 3.7 %fusion.124 = f32[160,1536]{1,0:T(8,128)S(1)} fusion(f32[160,1536]{1,0:T(8,128)S(1)} %copy.66, f32[160,1536]{1,0:T(8,128)} %get-tuple-element.272, bf16[1536,1536]{1,0:T(8,128)(2,1)} %get-tuple-element.270, f32[160,1536]{1,0:T(8,128)S(1)} %get-tuple-element.271, f32[1536]{0:T(1024)S(1)} %get-tuple-element.273, ...), kind=kOutput, calls=%fused_computation.13.clone.1 | convolution fusion | flops 757678080 | bytes 8657056 | tf_op jit(solution)/shard_map/while/body/eval_jaxpr/dot_general | solution.py:43
  82.4 3.7 %fusion.124 = f32[160,1536]{1,0:T(8,128)S(1)} fusion(f32[160,1536]{1,0:T(8,128)S(1)} %copy.66, f32[160,1536]{1,0:T(8,128)} %get-tuple-element.272, bf16[1536,1536]{1,0:T(8,128)(2,1)} %get-tuple-element.270, f32[160,1536]{1,0:T(8,128)S(1)} %get-tuple-element.271, f32[1536]{0:T(1024)S(1)} %get-tuple-element.273, ...), kind=kOutput, calls=%fused_computation.13.clone.1 | convolution fusion | flops 757678080 | bytes 8657056 | tf_op jit(solution)/shard_map/while/body/eval_jaxpr/dot_general | solution.py:43
  88.0 38.9 %all-reduce.2 = s32[32]{0:T(128)S(1)} all-reduce(s32[32]{0:T(128)S(1)} %dynamic-update-slice), channel_id=1, replica_groups=mesh['row'=4,'col'=8] {'row','col'}, use_global_device_ids=true, to_apply=%add.2 | all-reduce | flops 32 | bytes 256
  130.1 1.6 scatter_custom_fusion.4
  133.1 5.2 %all-to-all-start.1 = ((f32[32,6,1536]{2,1,0:T(8,128)}), f32[32,6,1536]{2,1,0:T(8,128)S(1)}, u32[]{:S(2)}, u32[]{:S(2)}) async-start(f32[32,6,1536]{2,1,0:T(8,128)} %all_to_all.19), calls=%async_computation.1 | async-start | bytes 3145728 | tf_op jit(solution)/shard_map/all_to_all | solution.py:147
  139.7 1.5 slice_multiply_fusion
  141.7 2.3 convolution_multiply_fusion.1
  144.1 1.4 stack.87
  145.5 1.7 fusion.9
  147.4 3.4 %scatter_custom_fusion.1 = f32[6,8192]{0,1:T(8,128)} fusion(s32[160]{0:T(256)} %copy-done.21, f32[160,6]{1,0:T(8,128)S(1)} %copy.29, f32[]{:T(128)} %constant.127.clone.1), kind=kCustom, calls=%fused_computation.24 | custom fusion | flops 960 | bytes 197120 | tf_op jit(solution)/shard_map/scatter-add | solution.py:162
  150.8 21.8 %slice_reduce_fusion = (f32[8192]{0:T(1024)}, f32[8192]{0:T(1024)S(1)}, f32[8192]{0:T(1024)S(1)}, f32[8192]{0:T(1024)S(1)}, f32[8192]{0:T(1024)}, /*index=5*/f32[8192]{0:T(1024)}) fusion(f32[6,8192]{0,1:T(8,128)} %scatter_custom_fusion.1), kind=kLoop, calls=%fused_computation.16 | loop fusion | bytes 393216 | tf_op jit(solution)/shard_map/slice | solution.py:71
  172.9 3.4 %scatter_custom_fusion.2 = f32[3,8192]{0,1:T(8,128)} fusion(s32[160]{0:T(256)} %copy-done.21, f32[160,3]{1,0:T(8,128)S(1)} %copy.30, f32[]{:T(128)} %constant.127.clone.1), kind=kCustom, calls=%fused_computation.22 | custom fusion | flops 480 | bytes 98816 | tf_op jit(solution)/shard_map/scatter-add | solution.py:156
  176.3 2.8 copy.31
  179.8 1.6 scatter_custom_fusion
  182.2 3.7 %collective-permute-start.5 = (f32[3,66,1]{2,1,0:T(8,128)S(1)}, f32[3,66,1]{2,1,0:T(8,128)S(1)}, u32[]{:S(2)}, u32[]{:S(2)}) collective-permute-start(f32[3,66,1]{2,1,0:T(8,128)S(1)} %get-tuple-element.190), channel_id=1, source_target_pairs={{0,1},{1,2},{2,3},{3,4},{4,5},{5,6},{6,7},{8,9},{9,10},{10,11},{11... | collective-permute-start | bytes 2384 | tf_op jit(solution)/shard_map/ppermute | solution.py:27
  188.5 4.1 %collective-permute-done.4 = f32[3,66,1]{2,1,0:T(8,128)S(1)} collective-permute-done((f32[3,66,1]{2,1,0:T(8,128)S(1)}, f32[3,66,1]{2,1,0:T(8,128)S(1)}, u32[]{:S(2)}, u32[]{:S(2)}) %collective-permute-start.4) | collective-permute-done | bytes 824 | tf_op jit(solution)/shard_map/ppermute | solution.py:29
  197.4 3.0 collective-permute-start.7
  201.4 4.3 %collective-permute-start.9 = (f32[6,66,1]{2,1,0:T(8,128)S(1)}, f32[6,66,1]{2,1,0:T(8,128)S(1)}, u32[]{:S(2)}, u32[]{:S(2)}) collective-permute-start(f32[6,66,1]{2,1,0:T(8,128)S(1)} %get-tuple-element.182), channel_id=1, source_target_pairs={{0,1},{1,2},{2,3},{3,4},{4,5},{5,6},{6,7},{8,9},{9,10},{10,11},{11... | collective-permute-start | bytes 4760 | tf_op jit(solution)/shard_map/ppermute | solution.py:27
  207.7 8.5 %collective-permute-done.9 = f32[6,66,1]{2,1,0:T(8,128)S(1)} collective-permute-done((f32[6,66,1]{2,1,0:T(8,128)S(1)}, f32[6,66,1]{2,1,0:T(8,128)S(1)}, u32[]{:S(2)}, u32[]{:S(2)}) %collective-permute-start.9) | collective-permute-done | bytes 1616 | tf_op jit(solution)/shard_map/ppermute | solution.py:27
  218.7 3.0 collective-permute-start.11
  223.4 4.4 %collective-permute-start.13 = (f32[6,66,1]{2,1,0:T(8,128)}, f32[6,66,1]{2,1,0:T(8,128)S(1)}, u32[]{:S(2)}, u32[]{:S(2)}) collective-permute-start(f32[6,66,1]{2,1,0:T(8,128)} %get-tuple-element.180), channel_id=1, source_target_pairs={{0,1},{1,2},{2,3},{3,4},{4,5},{5,6},{6,7},{8,9},{9,10},{10,11},{11... | collective-permute-start | bytes 4760 | tf_op jit(solution)/shard_map/ppermute | solution.py:27
  230.1 2.4 scatter_custom_fusion.3
  232.5 2.5 all_to_all.16
  235.7 2.5 collective-permute-done.12
  239.6 6.4 %all-to-all-start = ((f32[32,6,1536]{2,1,0:T(8,128)}), f32[32,6,1536]{2,1,0:T(8,128)}, u32[]{:S(2)}, u32[]{:S(2)}) async-start(f32[32,6,1536]{2,1,0:T(8,128)} %all_to_all.16), calls=%async_computation | async-start | bytes 3145728 | tf_op jit(solution)/shard_map/all_to_all | solution.py:146
  247.4 3.0 collective-permute-start.15
  251.4 3.6 %collective-permute-start.17 = (f32[6,66,1]{2,1,0:T(8,128)S(1)}, f32[6,66,1]{2,1,0:T(8,128)S(1)}, u32[]{:S(2)}, u32[]{:S(2)}) collective-permute-start(f32[6,66,1]{2,1,0:T(8,128)S(1)} %get-tuple-element.178), channel_id=1, source_target_pairs={{0,1},{1,2},{2,3},{3,4},{4,5},{5,6},{6,7},{8,9},{9,10},{10,11},{11... | collective-permute-start | bytes 4760 | tf_op jit(solution)/shard_map/ppermute | solution.py:27
  257.0 8.6 %collective-permute-done.17 = f32[6,66,1]{2,1,0:T(8,128)S(1)} collective-permute-done((f32[6,66,1]{2,1,0:T(8,128)S(1)}, f32[6,66,1]{2,1,0:T(8,128)S(1)}, u32[]{:S(2)}, u32[]{:S(2)}) %collective-permute-start.17) | collective-permute-done | bytes 1616 | tf_op jit(solution)/shard_map/ppermute | solution.py:27
  265.6 5.3 %collective-permute-done.16 = f32[6,66,1]{2,1,0:T(8,128)S(1)} collective-permute-done((f32[6,66,1]{2,1,0:T(8,128)S(1)}, f32[6,66,1]{2,1,0:T(8,128)S(1)}, u32[]{:S(2)}, u32[]{:S(2)}) %collective-permute-start.16) | collective-permute-done | bytes 1616 | tf_op jit(solution)/shard_map/ppermute | solution.py:29
  271.9 56.6 %all-reduce.3 = (f32[]{:T(128)}, f32[]{:T(128)}) all-reduce(f32[]{:T(128)} %get-tuple-element.136, f32[]{:T(128)} %get-tuple-element.135), channel_id=1, replica_groups=mesh['row'=4,'col'=8] {'row','col'}, use_global_device_ids=true, to_apply=%region_6.7 | all-reduce | flops 2 | bytes 16 | tf_op jit(solution)/shard_map/psum | solution.py:194
  331.5 1.6 all_to_all.18
  (189 shorter events, 40.3 us)
Async XLA Ops:
  0.6 20.9 %copy-start.1 = (f32[160,1536]{1,0:T(8,128)S(1)}, f32[160,1536]{1,0:T(8,128)}, u32[]{:S(2)}) copy-start(f32[160,1536]{1,0:T(8,128)} %param.23) | copy-start | bytes 2949124
  0.6 20.9 %copy-start.24 = (s32[160]{0:T(256)S(1)}, s32[160]{0:T(256)}, u32[]{:S(2)}) copy-start(s32[160]{0:T(256)} %param.25) | copy-start | bytes 1924
  2.0 179.4 %collective-permute-start.2 = (f32[3,1,128]{2,1,0:T(1,128)}, f32[3,1,128]{2,1,0:T(1,128)}, u32[]{:S(2)}, u32[]{:S(2)}) collective-permute-start(f32[3,1,128]{2,1,0:T(1,128)} %get-tuple-element.192), channel_id=1, source_target_pairs={{8,0},{16,8},{24,16},{9,1},{17,9},{25,17},{10,2},{18,10},{26,18},{... | collective-permute-start | bytes 4616 | tf_op jit(solution)/shard_map/ppermute | solution.py:29
  3.3 178.1 %collective-permute-start.3 = (f32[3,1,128]{2,1,0:T(1,128)}, f32[3,1,128]{2,1,0:T(1,128)}, u32[]{:S(2)}, u32[]{:S(2)}) collective-permute-start(f32[3,1,128]{2,1,0:T(1,128)} %get-tuple-element.191), channel_id=1, source_target_pairs={{0,8},{8,16},{16,24},{1,9},{9,17},{17,25},{2,10},{10,18},{18,26},{... | collective-permute-start | bytes 4616 | tf_op jit(solution)/shard_map/ppermute | solution.py:27
  8.3 5.0 %copy-start.3 = (f32[64,128]{1,0:T(8,128)}, f32[64,128]{1,0:T(8,128)S(1)}, u32[]{:S(2)}) copy-start(f32[64,128]{1,0:T(8,128)S(1)} %get-tuple-element.194) | copy-start | bytes 98308
  8.3 5.7 %copy-start.15 = (f32[1,64,128]{2,1,0:T(8,128)}, f32[1,64,128]{2,1,0:T(8,128)S(1)}, u32[]{:S(2)}) copy-start(f32[1,64,128]{2,1,0:T(8,128)S(1)} %get-tuple-element.195) | copy-start | bytes 98308
  8.9 178.4 %collective-permute-start = (f32[1,128]{1,0:T(1,128)}, f32[1,128]{1,0:T(1,128)}, u32[]{:S(2)}, u32[]{:S(2)}) collective-permute-start(f32[1,128]{1,0:T(1,128)} %slice_bitcast_fusion.22), channel_id=1, source_target_pairs={{0,8},{8,16},{16,24},{1,9},{9,17},{17,25},{2,10},{10,18},{18,26},{... | collective-permute-start | bytes 1544 | tf_op jit(solution)/shard_map/ppermute | solution.py:16
  14.0 173.2 %collective-permute-start.1 = (f32[64,1]{1,0:T(8,128)}, f32[64,1]{1,0:T(8,128)}, u32[]{:S(2)}, u32[]{:S(2)}) collective-permute-start(f32[64,1]{1,0:T(8,128)} %slice.472), channel_id=1, source_target_pairs={{0,1},{1,2},{2,3},{3,4},{4,5},{5,6},{6,7},{8,9},{9,10},{10,11},{11... | collective-permute-start | bytes 776 | tf_op jit(solution)/shard_map/ppermute | solution.py:16
  21.4 25.0 %copy-start.17 = (s32[160]{0:T(256)S(1)}, s32[160]{0:T(256)}, u32[]{:S(2)}) copy-start(s32[160]{0:T(256)} %param.24) | copy-start | bytes 1924
  21.4 28.5 %copy-start.14 = (f32[3,1536]{1,0:T(4,128)S(1)}, f32[3,1536]{1,0:T(4,128)}, u32[]{:S(2)}) copy-start(f32[3,1536]{1,0:T(4,128)} %param.21) | copy-start | bytes 55300
  21.4 30.3 %copy-start = (f32[160,1536]{1,0:T(8,128)S(1)}, f32[160,1536]{1,0:T(8,128)}, u32[]{:S(2)}) copy-start(f32[160,1536]{1,0:T(8,128)} %param.22) | copy-start | bytes 2949124
  127.8 1.3 copy-start.27
  130.1 3.0 copy-start.23
  133.1 106.5 %all-to-all-start.1 = ((f32[32,6,1536]{2,1,0:T(8,128)}), f32[32,6,1536]{2,1,0:T(8,128)S(1)}, u32[]{:S(2)}, u32[]{:S(2)}) async-start(f32[32,6,1536]{2,1,0:T(8,128)} %all_to_all.19), calls=%async_computation.1 | async-start | bytes 3145728 | tf_op jit(solution)/shard_map/all_to_all | solution.py:147
  138.3 3.4 %copy-start.20 = (f32[160]{0:T(256)}, f32[160]{0:T(256)S(1)}, u32[]{:S(2)}) copy-start(f32[160]{0:T(256)S(1)} %broadcast_select_fusion.2) | copy-start | bytes 1924
  150.8 21.8 %copy-start.28 = (s32[32]{0:T(128)S(1)}, s32[32]{0:T(128)}, u32[]{:S(2)}) copy-start(s32[32]{0:T(128)} %copy-done.27) | copy-start | bytes 388
  150.8 21.8 %copy-start.29 = (s32[80]{0:T(128)S(1)}, s32[80]{0:T(128)}, u32[]{:S(2)}) copy-start(s32[80]{0:T(128)} %fusion.85) | copy-start | bytes 964
  150.8 21.9 %copy-start.19 = (f32[160,3]{0,1:T(4,128)S(1)}, f32[160,3]{0,1:T(4,128)}, u32[]{:S(2)}) copy-start(f32[160,3]{0,1:T(4,128)} %convolution_multiply_fusion.1) | copy-start | bytes 5764
  172.7 27.7 %copy-start.25 = (s32[80]{0:T(128)}, s32[80]{0:T(128)S(1)}, u32[]{:S(2)}) copy-start(s32[80]{0:T(128)S(1)} %convert_reduce_fusion) | copy-start | bytes 964
  172.8 8.6 %copy-start.5 = (f32[3,64,128]{2,1,0:T(8,128)S(1)}, f32[3,64,128]{2,1,0:T(8,128)}, u32[]{:S(2)}) copy-start(f32[3,64,128]{2,1,0:T(8,128)} %param.14) | copy-start | bytes 294916
  172.8 14.4 %copy-start.4 = (f32[64,128]{1,0:T(8,128)S(1)}, f32[64,128]{1,0:T(8,128)}, u32[]{:S(2)}) copy-start(f32[64,128]{1,0:T(8,128)} %copy-done.3) | copy-start | bytes 98308
  172.8 14.4 %copy-start.12 = (s32[2,64,128]{2,1,0:T(8,128)S(1)}, s32[2,64,128]{2,1,0:T(8,128)}, u32[]{:S(2)}) copy-start(s32[2,64,128]{2,1,0:T(8,128)} %param.17) | copy-start | bytes 196612
  172.9 14.4 %copy-start.16 = (f32[63,128]{1,0:T(8,128)S(1)}, f32[63,128]{1,0:T(8,128)}, u32[]{:S(2)}) copy-start(f32[63,128]{1,0:T(8,128)} %slice_bitcast_fusion.21) | copy-start | bytes 96772
  172.9 14.4 %copy-start.18 = (f32[64,128]{1,0:T(8,128)S(1)}, f32[64,128]{1,0:T(8,128)}, u32[]{:S(2)}) copy-start(f32[64,128]{1,0:T(8,128)} %param.16) | copy-start | bytes 98308
  172.9 19.7 %copy-start.2 = (f32[3,64,128]{2,1,0:T(8,128)S(1)}, f32[3,64,128]{2,1,0:T(8,128)}, u32[]{:S(2)}) copy-start(f32[3,64,128]{2,1,0:T(8,128)} %param.15) | copy-start | bytes 294916
  172.9 19.7 %copy-start.6 = (f32[64,128]{1,0:T(8,128)S(1)}, f32[64,128]{1,0:T(8,128)}, u32[]{:S(2)}) copy-start(f32[64,128]{1,0:T(8,128)} %get-tuple-element.193) | copy-start | bytes 98308
  182.2 6.3 %collective-permute-start.5 = (f32[3,66,1]{2,1,0:T(8,128)S(1)}, f32[3,66,1]{2,1,0:T(8,128)S(1)}, u32[]{:S(2)}, u32[]{:S(2)}) collective-permute-start(f32[3,66,1]{2,1,0:T(8,128)S(1)} %get-tuple-element.190), channel_id=1, source_target_pairs={{0,1},{1,2},{2,3},{3,4},{4,5},{5,6},{6,7},{8,9},{9,10},{10,11},{11... | collective-permute-start | bytes 2384 | tf_op jit(solution)/shard_map/ppermute | solution.py:27
  185.9 6.7 %collective-permute-start.4 = (f32[3,66,1]{2,1,0:T(8,128)S(1)}, f32[3,66,1]{2,1,0:T(8,128)S(1)}, u32[]{:S(2)}, u32[]{:S(2)}) collective-permute-start(f32[3,66,1]{2,1,0:T(8,128)S(1)} %get-tuple-element.189), channel_id=1, source_target_pairs={{1,0},{2,1},{3,2},{4,3},{5,4},{6,5},{7,6},{9,8},{10,9},{11,10},{12... | collective-permute-start | bytes 2384 | tf_op jit(solution)/shard_map/ppermute | solution.py:29
  188.1 29.2 %copy-start.8 = (f32[64,128]{1,0:T(8,128)}, f32[64,128]{1,0:T(8,128)S(1)}, u32[]{:S(2)}) copy-start(f32[64,128]{1,0:T(8,128)S(1)} %get-tuple-element.167) | copy-start | bytes 98308
  188.2 29.2 %copy-start.10 = (f32[64,128]{1,0:T(8,128)}, f32[64,128]{1,0:T(8,128)S(1)}, u32[]{:S(2)}) copy-start(f32[64,128]{1,0:T(8,128)S(1)} %get-tuple-element.168) | copy-start | bytes 98308
  196.1 4.4 %collective-permute-start.6 = (f32[6,1,128]{2,1,0:T(1,128)S(1)}, f32[6,1,128]{2,1,0:T(1,128)S(1)}, u32[]{:S(2)}, u32[]{:S(2)}) collective-permute-start(f32[6,1,128]{2,1,0:T(1,128)S(1)} %get-tuple-element.188), channel_id=1, source_target_pairs={{8,0},{16,8},{24,16},{9,1},{17,9},{25,17},{10,2},{18,10},{26,18},{... | collective-permute-start | bytes 9224 | tf_op jit(solution)/shard_map/ppermute | solution.py:29
  197.4 3.8 %collective-permute-start.7 = (f32[6,1,128]{2,1,0:T(1,128)S(1)}, f32[6,1,128]{2,1,0:T(1,128)S(1)}, u32[]{:S(2)}, u32[]{:S(2)}) collective-permute-start(f32[6,1,128]{2,1,0:T(1,128)S(1)} %get-tuple-element.187), channel_id=1, source_target_pairs={{0,8},{8,16},{16,24},{1,9},{9,17},{17,25},{2,10},{10,18},{18,26},{... | collective-permute-start | bytes 9224 | tf_op jit(solution)/shard_map/ppermute | solution.py:27
  200.5 21.3 %copy-start.22 = (s32[80]{0:T(128)}, s32[80]{0:T(128)S(1)}, u32[]{:S(2)}) copy-start(s32[80]{0:T(128)S(1)} %broadcast_add_fusion) | copy-start | bytes 964
  201.4 14.8 %collective-permute-start.9 = (f32[6,66,1]{2,1,0:T(8,128)S(1)}, f32[6,66,1]{2,1,0:T(8,128)S(1)}, u32[]{:S(2)}, u32[]{:S(2)}) collective-permute-start(f32[6,66,1]{2,1,0:T(8,128)S(1)} %get-tuple-element.182), channel_id=1, source_target_pairs={{0,1},{1,2},{2,3},{3,4},{4,5},{5,6},{6,7},{8,9},{9,10},{10,11},{11... | collective-permute-start | bytes 4760 | tf_op jit(solution)/shard_map/ppermute | solution.py:27
  205.7 10.5 %collective-permute-start.8 = (f32[6,66,1]{2,1,0:T(8,128)S(1)}, f32[6,66,1]{2,1,0:T(8,128)S(1)}, u32[]{:S(2)}, u32[]{:S(2)}) collective-permute-start(f32[6,66,1]{2,1,0:T(8,128)S(1)} %get-tuple-element.181), channel_id=1, source_target_pairs={{1,0},{2,1},{3,2},{4,3},{5,4},{6,5},{7,6},{9,8},{10,9},{11,10},{12... | collective-permute-start | bytes 4760 | tf_op jit(solution)/shard_map/ppermute | solution.py:29
  217.4 5.2 %collective-permute-start.10 = (f32[6,1,128]{2,1,0:T(1,128)S(1)}, f32[6,1,128]{2,1,0:T(1,128)S(1)}, u32[]{:S(2)}, u32[]{:S(2)}) collective-permute-start(f32[6,1,128]{2,1,0:T(1,128)S(1)} %get-tuple-element.186), channel_id=1, source_target_pairs={{8,0},{16,8},{24,16},{9,1},{17,9},{25,17},{10,2},{18,10},{26,18},{... | collective-permute-start | bytes 9224 | tf_op jit(solution)/shard_map/ppermute | solution.py:29
  218.7 3.9 %collective-permute-start.11 = (f32[6,1,128]{2,1,0:T(1,128)S(1)}, f32[6,1,128]{2,1,0:T(1,128)S(1)}, u32[]{:S(2)}, u32[]{:S(2)}) collective-permute-start(f32[6,1,128]{2,1,0:T(1,128)S(1)} %get-tuple-element.185), channel_id=1, source_target_pairs={{0,8},{8,16},{16,24},{1,9},{9,17},{17,25},{2,10},{10,18},{18,26},{... | collective-permute-start | bytes 9224 | tf_op jit(solution)/shard_map/ppermute | solution.py:27
  223.4 11.6 %collective-permute-start.13 = (f32[6,66,1]{2,1,0:T(8,128)}, f32[6,66,1]{2,1,0:T(8,128)S(1)}, u32[]{:S(2)}, u32[]{:S(2)}) collective-permute-start(f32[6,66,1]{2,1,0:T(8,128)} %get-tuple-element.180), channel_id=1, source_target_pairs={{0,1},{1,2},{2,3},{3,4},{4,5},{5,6},{6,7},{8,9},{9,10},{10,11},{11... | collective-permute-start | bytes 4760 | tf_op jit(solution)/shard_map/ppermute | solution.py:27
  227.8 10.4 %collective-permute-start.12 = (f32[6,66,1]{2,1,0:T(8,128)}, f32[6,66,1]{2,1,0:T(8,128)}, u32[]{:S(2)}, u32[]{:S(2)}) collective-permute-start(f32[6,66,1]{2,1,0:T(8,128)} %get-tuple-element.179), channel_id=1, source_target_pairs={{1,0},{2,1},{3,2},{4,3},{5,4},{6,5},{7,6},{9,8},{10,9},{11,10},{12... | collective-permute-start | bytes 4760 | tf_op jit(solution)/shard_map/ppermute | solution.py:29
  232.5 18.0 %copy-start.26 = (s32[80]{0:T(128)S(1)}, s32[80]{0:T(128)}, u32[]{:S(2)}) copy-start(s32[80]{0:T(128)} %copy-done.25) | copy-start | bytes 964
  235.0 35.9 %copy-start.7 = (f32[64,128]{1,0:T(8,128)S(1)}, f32[64,128]{1,0:T(8,128)}, u32[]{:S(2)}) copy-start(f32[64,128]{1,0:T(8,128)} %get-tuple-element.193) | copy-start | bytes 98308
  235.0 35.9 %copy-start.9 = (f32[64,128]{1,0:T(8,128)S(1)}, f32[64,128]{1,0:T(8,128)}, u32[]{:S(2)}) copy-start(f32[64,128]{1,0:T(8,128)} %copy-done.8) | copy-start | bytes 98308
  235.0 35.9 %copy-start.11 = (f32[64,128]{1,0:T(8,128)S(1)}, f32[64,128]{1,0:T(8,128)}, u32[]{:S(2)}) copy-start(f32[64,128]{1,0:T(8,128)} %copy-done.10) | copy-start | bytes 98308
  239.6 91.8 %all-to-all-start = ((f32[32,6,1536]{2,1,0:T(8,128)}), f32[32,6,1536]{2,1,0:T(8,128)}, u32[]{:S(2)}, u32[]{:S(2)}) async-start(f32[32,6,1536]{2,1,0:T(8,128)} %all_to_all.16), calls=%async_computation | async-start | bytes 3145728 | tf_op jit(solution)/shard_map/all_to_all | solution.py:146
  246.1 5.0 %collective-permute-start.14 = (f32[6,1,128]{2,1,0:T(1,128)S(1)}, f32[6,1,128]{2,1,0:T(1,128)S(1)}, u32[]{:S(2)}, u32[]{:S(2)}) collective-permute-start(f32[6,1,128]{2,1,0:T(1,128)S(1)} %get-tuple-element.184), channel_id=1, source_target_pairs={{8,0},{16,8},{24,16},{9,1},{17,9},{25,17},{10,2},{18,10},{26,18},{... | collective-permute-start | bytes 9224 | tf_op jit(solution)/shard_map/ppermute | solution.py:29
  247.4 3.8 %collective-permute-start.15 = (f32[6,1,128]{2,1,0:T(1,128)S(1)}, f32[6,1,128]{2,1,0:T(1,128)S(1)}, u32[]{:S(2)}, u32[]{:S(2)}) collective-permute-start(f32[6,1,128]{2,1,0:T(1,128)S(1)} %get-tuple-element.183), channel_id=1, source_target_pairs={{0,8},{8,16},{16,24},{1,9},{9,17},{17,25},{2,10},{10,18},{18,26},{... | collective-permute-start | bytes 9224 | tf_op jit(solution)/shard_map/ppermute | solution.py:27
  251.4 14.2 %collective-permute-start.17 = (f32[6,66,1]{2,1,0:T(8,128)S(1)}, f32[6,66,1]{2,1,0:T(8,128)S(1)}, u32[]{:S(2)}, u32[]{:S(2)}) collective-permute-start(f32[6,66,1]{2,1,0:T(8,128)S(1)} %get-tuple-element.178), channel_id=1, source_target_pairs={{0,1},{1,2},{2,3},{3,4},{4,5},{5,6},{6,7},{8,9},{9,10},{10,11},{11... | collective-permute-start | bytes 4760 | tf_op jit(solution)/shard_map/ppermute | solution.py:27
  255.1 15.9 %collective-permute-start.16 = (f32[6,66,1]{2,1,0:T(8,128)S(1)}, f32[6,66,1]{2,1,0:T(8,128)S(1)}, u32[]{:S(2)}, u32[]{:S(2)}) collective-permute-start(f32[6,66,1]{2,1,0:T(8,128)S(1)} %get-tuple-element.177), channel_id=1, source_target_pairs={{1,0},{2,1},{3,2},{4,3},{5,4},{6,5},{7,6},{9,8},{10,9},{11,10},{12... | collective-permute-start | bytes 4760 | tf_op jit(solution)/shard_map/ppermute | solution.py:29
  (2 other events, 1.2 us)
where the time goes:
time: 339 us; the launch traced here: 336 us
  blocking collectives  95.5 us (28%)
  local copies, waits for them, and re-layouts  75.1 us (22%)
  starting transfers between devices  59.2 us (17%)
  matrix products  39.3 us (12%)
  other arithmetic  31.1 us (9%)
  waiting for transfers between devices  30.3 us (9%)
  between operations  5.37 us (2%)
    psum x1, blocking collectives, on_device(): lax.psum((jnp.sum(correction * direction), jnp.sum(direction * direction)...  56.6 us
    unnamed x1, blocking collectives  38.9 us
    dot_general x9, matrix products, advance(): jnp.dot(current.astype(jnp.bfloat16), stiffness, preferred_element_type=j...  33.4 us
    ppermute x8, starting transfers between devices, extended(): lax.ppermute(tail, axis, [(i, (i + 1) % count) for i in range(ends)])  28.7 us
    gather x1, local copies, waits for them, and re-layouts, micro_solve(): diagonal = jnp.diagonal(stiffness).astype(jnp.float32)  24.3 us
    slice x1, local copies, waits for them, and re-layouts, block_solve(): d00 = scale + tangent[0]  21.8 us
    ppermute x8, waiting for transfers between devices, extended(): lax.ppermute(tail, axis, [(i, (i + 1) % count) for i in range(ends)])  18.3 us
    ppermute x8, waiting for transfers between devices, extended(): lax.ppermute(head, axis, [((i + 1) % count, i) for i in range(ends)])  12 us
  transfers between devices with their start and end apart: 20, of which 8 were waited for; matrix products, arithmetic and copies ran while one was open for 40% of the time, Pallas kernels for 0%

commit v1 on v0

v1 whole, which is shorter than its diff:
```python
import functools

import jax
import jax.numpy as jnp
from jax import lax
from jax.experimental import pallas as pl
from jax.experimental.pallas import tpu as pltpu
from jax.sharding import PartitionSpec as P

MAX_STEPS = 9
SWEEPS = 3
TILE = 256
LANES = 128
MESH = pl.DeviceIdType.MESH
F32 = jnp.float32
BF16 = jnp.bfloat16
HIGHEST = lax.Precision.HIGHEST


def iota(shape, dim):
    return lax.broadcasted_iota(jnp.int32, shape, dim)


def picked(onehot, values):
    high = values.astype(BF16)
    rest = values - high.astype(F32)
    middle = rest.astype(BF16)
    low = (rest - middle.astype(F32)).astype(BF16)
    dot = functools.partial(jnp.dot, preferred_element_type=F32)
    return dot(onehot, high) + dot(onehot, middle) + dot(onehot, low)


def body(
    nrow,
    ncol,
    pair,
    jump_ref,
    external_ref,
    cohesive_ref,
    bond_ref,
    load_ref,
    radius_ref,
    coupling_ref,
    steps_ref,
    points_ref,
    stiffness_hbm,
    state_hbm,
    history_hbm,
    new_jump_ref,
    new_load_ref,
    new_state_ref,
    new_history_ref,
    stiff,
    state,
    history,
    damage,
    load,
    rounded,
    diagonal,
    count_out,
    count_in,
    sum_out,
    sum_in,
    x_out,
    x_in,
    y_out,
    y_in,
    out_history,
    in_history,
    out_state,
    in_state,
    local_sems,
    halo_send,
    halo_recv,
    all_send,
    all_recv,
):
    devices = nrow * ncol
    row, col = lax.axis_index("row"), lax.axis_index("col")
    here = row * ncol + col
    slots, cells = state.shape
    X, Y = cohesive_ref.shape
    new_cap = new_state_ref.shape[0]
    padded = out_history.shape[1]
    width = devices * padded
    bits = devices.bit_length() - 1

    fetch = [
        pltpu.make_async_copy(history_hbm, history, local_sems.at[0]),
        pltpu.make_async_copy(stiffness_hbm, stiff, local_sems.at[1]),
        pltpu.make_async_copy(state_hbm, state, local_sems.at[2]),
    ]
    for copy in fetch:
        copy.start()

    def peer(k):
        p = lax.rem(here + k, devices)
        return {"row": lax.div(p, ncol), "col": lax.rem(p, ncol)}, p

    x_in[...] = jnp.zeros_like(x_in)
    y_in[...] = jnp.zeros_like(y_in)
    if pair < padded:
        blank = jnp.zeros((devices, padded - pair, cells), F32)
        in_history[:, pair:, :] = blank
        in_state[:, pair:, :] = blank

    steps_row = steps_ref[...]
    live_row = (steps_row > 0).astype(F32)
    count_out[...] = jnp.broadcast_to(jnp.sum(live_row, axis=1, keepdims=True), count_out.shape)

    lane = iota((X, Y), 1)
    line = iota((X, Y), 0)

    def stage(phase, fields):
        right = jnp.zeros((X, Y), F32)
        left = jnp.zeros((X, Y), F32)
        for c, (x_field, y_field) in enumerate(fields):
            x_out[phase, 0, c : c + 1, :] = x_field[X - 1 : X, :]
            x_out[phase, 1, c : c + 1, :] = x_field[0:1, :]
            right = jnp.where(lane == c, pltpu.roll(y_field, (c + 1) % Y, 1), right)
            left = jnp.where(lane == c, pltpu.roll(y_field, c, 1), left)
        y_out[phase, 0] = right
        y_out[phase, 1] = left

    def halo_copies(phase):
        plan = (
            (x_out, x_in, 0, row < nrow - 1, row > 0, {"row": row + 1, "col": col}),
            (x_out, x_in, 1, row > 0, row < nrow - 1, {"row": row - 1, "col": col}),
            (y_out, y_in, 0, col < ncol - 1, col > 0, {"row": row, "col": col + 1}),
            (y_out, y_in, 1, col > 0, col < ncol - 1, {"row": row, "col": col - 1}),
        )
        copies = []
        for index, (source, target, way, sends, gets, device) in enumerate(plan):
            copy = pltpu.make_async_remote_copy(
                src_ref=source.at[phase, way],
                dst_ref=target.at[phase, way],
                send_sem=halo_send.at[phase, index],
                recv_sem=halo_recv.at[phase, index],
                device_id=device,
                device_id_type=MESH,
            )
            copies.append((copy, sends, gets))
        return copies

    def halo_start(phase):
        for copy, sends, _ in halo_copies(phase):
            pl.when(sends)(copy.start)

    def halo_wait(phase):
        for copy, sends, gets in halo_copies(phase):
            pl.when(gets)(copy.wait_recv)

    def halo_wait_sends(phase):
        for copy, sends, gets in halo_copies(phase):
            pl.when(sends)(copy.wait_send)

    def spread(source_of, target, kind, first, last):
        def one(k, carry):
            device, p = peer(k)
            pltpu.make_async_remote_copy(
                src_ref=source_of(p),
                dst_ref=target,
                send_sem=all_send.at[kind],
                recv_sem=all_recv.at[kind],
                device_id=device,
                device_id_type=MESH,
            ).start()
            return carry

        lax.fori_loop(first, last, one, 0)

    def spread_wait(buffer, sem):
        pltpu.make_async_copy(buffer, buffer, sem).wait()

    bond_x = 0.25 + 0.75 * bond_ref[0].astype(F32)
    bond_y = 0.25 + 0.75 * bond_ref[1].astype(F32)
    jump = [jump_ref[c] for c in range(3)]
    stage(0, [(jump[c], jump[c]) for c in range(3)] + [(bond_x, bond_y)])

    barrier = pltpu.get_barrier_semaphore()

    def greet(k, carry):
        device, _ = peer(k)
        pl.semaphore_signal(barrier, inc=1, device_id=device, device_id_type=MESH)
        return carry

    lax.fori_loop(1, devices, greet, 0)
    pl.semaphore_wait(barrier, devices - 1)

    count_in[pl.ds(here, 1)] = count_out[...][None]
    spread(lambda p: count_out, count_in.at[here], 0, 1, devices)
    halo_start(0)

    slot_line = iota((slots, slots), 0)
    slot_lane = iota((slots, slots), 1)

    def to_column(values):
        return jnp.sum(jnp.where(slot_line == slot_lane, values, 0.0), axis=1, keepdims=True)

    points_row = points_ref[...]
    px_row = lax.shift_right_logical(points_row, (Y.bit_length() - 1))
    py_row = points_row & (Y - 1)
    px_col = to_column(px_row.astype(F32)).astype(jnp.int32)
    py_col = to_column(py_row.astype(F32)).astype(jnp.int32)
    steps_col = to_column(steps_row.astype(F32)).astype(jnp.int32)
    live_col = (steps_col > 0).astype(F32)
    at_x = (iota((slots, X), 1) == px_col).astype(F32)
    at_y = (iota((slots, Y), 1) == py_col).astype(F32)
    at_x_turned = (iota((X, slots), 0) == px_row).astype(F32)
    drive = []
    for c in range(3):
        lines = jnp.dot(at_x, jump[c], precision=HIGHEST, preferred_element_type=F32)
        drive.append(jnp.sum(lines * at_y, axis=1, keepdims=True))
    for start in range(0, cells, TILE):
        part = slice(start, start + TILE)
        total = drive[0] * coupling_ref[0:1, part]
        total = total + drive[1] * coupling_ref[1:2, part]
        load[:, part] = total + drive[2] * coupling_ref[2:3, part]
    rank_row = jnp.sum(jnp.where(slot_line < slot_lane, live_col, 0.0), axis=0, keepdims=True)

    fetch[0].wait()
    for start in range(0, cells, TILE):
        part = slice(start, start + TILE)
        damage[:, part] = jnp.exp(-history[:, part])

    spread_wait(count_in.at[pl.ds(0, devices - 1)], all_recv.at[0])
    counts = jnp.max(count_in[...], axis=1)
    device_line = iota((devices, LANES), 0)
    device_lane = iota((devices, LANES), 1)
    starts = jnp.sum(jnp.where(device_line < device_lane, counts, 0.0), axis=0, keepdims=True)
    ends = jnp.sum(jnp.where(device_line <= device_lane, counts, 0.0), axis=0, keepdims=True)
    my_start = jnp.sum(jnp.where(device_line < here, counts, 0.0), axis=0, keepdims=True)[:, :1]
    my_start = my_start.astype(jnp.int32)

    def place(rank, first):
        pairs = lax.shift_right_logical(rank, 1) - lax.shift_right_logical(first, 1)
        return 2 * lax.shift_right_logical(pairs, bits) + (rank & 1)

    ranks = rank_row.astype(jnp.int32) + my_start
    home = lax.shift_right_logical(ranks, 1) & (devices - 1)
    leaves = jnp.where(steps_row > 0, home * padded + place(ranks, my_start), -1)
    leaving = (iota((width, slots), 0) == leaves).astype(F32).astype(BF16)

    wanted_slot = iota((new_cap, LANES), 0)
    wanted = 2 * (here + devices * lax.shift_right_logical(wanted_slot, 1)) + (wanted_slot & 1)
    wanted_lane = iota((new_cap, LANES), 1)
    wanted_float = wanted.astype(F32)
    hit = (starts <= wanted_float) & (wanted_float < ends) & (wanted_lane < devices)
    valid = jnp.sum(jnp.where(hit, 1.0, 0.0), axis=1, keepdims=True)
    from_start = jnp.sum(jnp.where(hit, starts, 0.0), axis=1, keepdims=True).astype(jnp.int32)
    source = jnp.sum(jnp.where(hit, wanted_lane.astype(F32), 0.0), axis=1, keepdims=True)
    arrives = source.astype(jnp.int32) * padded + place(wanted[:, :1], from_start)
    arrives = jnp.where(valid > 0.0, arrives, -1)
    coming = (iota((new_cap, width), 1) == arrives).astype(F32).astype(BF16)

    def gather_out(values, out, inside):
        for start in range(0, cells, TILE):
            part = slice(start, start + TILE)
            rows = picked(leaving, values[:, part])
            out[:, :, part] = rows.reshape(devices, padded, TILE)
        inside[pl.ds(here, 1)] = out[pl.ds(here, 1)]

    gather_out(history, out_history, in_history)
    row_part = pl.ds(0, pair)
    spread(
        lambda p: out_history.at[p, row_part], in_history.at[here, row_part], 1, 1, devices
    )

    fetch[1].wait()
    fetch[2].wait()
    tile_eye = iota((TILE, TILE), 0) == iota((TILE, TILE), 1)
    for start in range(0, cells, TILE):
        part = slice(start, start + TILE)
        block = stiff[part, part].astype(F32)
        diagonal[:, part] = jnp.sum(jnp.where(tile_eye, block, 0.0), axis=0, keepdims=True)
        rounded[0, :, part] = state[:, part].astype(BF16)

    def advance(count, carry):
        now = lax.rem(count, 2)
        moves = count < steps_col
        for start in range(0, cells, TILE):
            part = slice(start, start + TILE)
            force = jnp.dot(rounded[now], stiff[:, part], preferred_element_type=F32)
            current = state[:, part]
            bent = jnp.tanh(current)
            worn = damage[:, part]
            misfit = force + worn * bent - load[:, part]
            slope = diagonal[:, part] + worn * (1.0 - bent * bent)
            current = jnp.where(moves, current - misfit / slope, current)
            state[:, part] = current
            rounded[1 - now, :, part] = current.astype(BF16)
        return carry

    lax.fori_loop(0, MAX_STEPS, advance, 0)

    first_sum = jnp.zeros((slots, 8), F32)
    second_sum = jnp.zeros((slots, 8), F32)
    turned = (((1,), (1,)), ((), ()))
    for start in range(0, cells, TILE):
        part = slice(start, start + TILE)
        bent = jnp.tanh(state[:, part])
        worn = damage[:, part]
        a0, a1, a2 = [coupling_ref[a : a + 1, part] for a in range(3)]
        none = jnp.zeros((2, TILE), F32)
        firsts = jnp.concatenate([a0, a1, a2, none, none, none[:1]], axis=0)
        seconds = jnp.concatenate(
            [a0 * a0, a1 * a1, a2 * a2, a0 * a1, a0 * a2, a1 * a2, none], axis=0
        )
        first_sum = first_sum + lax.dot_general(
            worn * bent, firsts, turned, precision=HIGHEST, preferred_element_type=F32
        )
        second_sum = second_sum + lax.dot_general(
            worn * (1.0 - bent * bent),
            seconds,
            turned,
            precision=HIGHEST,
            preferred_element_type=F32,
        )
    first_sum = first_sum * (live_col / cells)
    second_sum = second_sum * (live_col / cells)

    def put(values):
        return jnp.dot(at_x_turned, at_y * values, precision=HIGHEST, preferred_element_type=F32)

    soft = put(live_col)
    rve_traction = [put(first_sum[:, c : c + 1]) for c in range(3)]
    tangent = [put(second_sum[:, c : c + 1]) for c in range(6)]

    halo_wait(0)

    def before_x(phase, field, c):
        return jnp.where(line == 0, x_in[phase, 0, c : c + 1, :], pltpu.roll(field, 1, 0))

    def after_x(phase, field, c):
        return jnp.where(line == X - 1, x_in[phase, 1, c : c + 1, :], pltpu.roll(field, X - 1, 0))

    def before_y(phase, field, c):
        edge = pltpu.roll(y_in[phase, 0], (Y - c) % Y, 1)
        return jnp.where(lane == 0, edge, pltpu.roll(field, 1, 1))

    def after_y(phase, field, c):
        edge = pltpu.roll(y_in[phase, 1], Y - 1 - c, 1)
        return jnp.where(lane == Y - 1, edge, pltpu.roll(field, Y - 1, 1))

    low_x = before_x(0, bond_x, 3)
    low_y = before_y(0, bond_y, 3)

    def neighbours(phase, field, c):
        return (
            bond_x * after_x(phase, field, c)
            + low_x * before_x(phase, field, c)
            + bond_y * after_y(phase, field, c)
            + low_y * before_y(phase, field, c)
        )

    scale = bond_x + low_x + bond_y + low_y + (1.0 - soft) * cohesive_ref[...]
    terms = []
    for c in range(3):
        residual = (
            scale * jump[c]
            - neighbours(0, jump[c], c)
            + rve_traction[c]
            - load_ref[0] * external_ref[c]
        )
        terms.append(-residual)
    for c in range(3):
        terms.append(external_ref[c])
    d00, d11, d22 = [scale + tangent[c] for c in range(3)]
    d01, d02, d12 = tangent[3:]
    c00 = d11 * d22 - d12 * d12
    c11 = d00 * d22 - d02 * d02
    c22 = d00 * d11 - d01 * d01
    c01 = d02 * d12 - d01 * d22
    c02 = d01 * d12 - d02 * d11
    c12 = d01 * d02 - d00 * d12
    inverse = 1.0 / (d00 * c00 + d01 * c01 + d02 * c02)
    c00, c11, c22, c01, c02, c12 = [c * inverse for c in (c00, c11, c22, c01, c02, c12)]

    def solve_both(w):
        result = []
        for h in (0, 3):
            result.append(c00 * w[h] + c01 * w[h + 1] + c02 * w[h + 2])
            result.append(c01 * w[h] + c11 * w[h + 1] + c12 * w[h + 2])
            result.append(c02 * w[h] + c12 * w[h + 1] + c22 * w[h + 2])
        return result

    iterate = solve_both(terms)
    bounds = [1 + (devices - 1) * s // SWEEPS for s in range(SWEEPS + 1)]
    for sweep in range(SWEEPS):
        phase = sweep + 1
        stage(phase, [(v, v) for v in iterate])
        halo_start(phase)
        if sweep == 0:
            gather_out(state, out_state, in_state)
        spread(
            lambda p: out_state.at[p, row_part],
            in_state.at[here, row_part],
            2,
            bounds[sweep],
            bounds[sweep + 1],
        )
        halo_wait(phase)
        iterate = solve_both([terms[c] + neighbours(phase, iterate[c], c) for c in range(6)])
    correction, direction = iterate[:3], iterate[3:]

    def total_of(fields):
        return jnp.sum(fields[0] + fields[1] + fields[2], axis=0, keepdims=True)

    cross_row = total_of([correction[c] * direction[c] for c in range(3)])
    square_row = total_of([direction[c] * direction[c] for c in range(3)])
    sum_out[...] = jnp.where(iota((8, Y), 0) == 0, cross_row, square_row)
    sum_in[pl.ds(here, 1)] = sum_out[...][None]
    spread(lambda p: sum_out, sum_in.at[here], 3, 1, devices)
    spread_wait(sum_in.at[pl.ds(0, devices - 1)], all_recv.at[3])
    sums = jnp.sum(sum_in[...], axis=0)
    cross = jnp.sum(sums[0:1, :], axis=1, keepdims=True)
    square = jnp.sum(sums[1:2, :], axis=1, keepdims=True)
    entries = 3.0 * X * Y * devices
    shifted = square + 0.25 * entries
    root = jnp.sqrt(shifted) * (entries**0.5)
    increment = (radius_ref[0] * root - cross) / shifted
    for c in range(3):
        new_jump_ref[c] = jump[c] + correction[c] + increment * direction[c]
    new_load_ref[...] = load_ref[0] + increment

    peers = pl.ds(0, devices - 1)
    spread_wait(in_history.at[peers, row_part], all_recv.at[1])
    spread_wait(in_state.at[peers, row_part], all_recv.at[2])
    for start in range(0, cells, TILE):
        part = slice(start, start + TILE)
        moved = picked(coming, in_state[:, :, part].reshape(width, TILE))
        kept = picked(coming, in_history[:, :, part].reshape(width, TILE))
        new_state_ref[:, part] = moved
        new_history_ref[:, part] = jnp.maximum(kept, jnp.abs(moved))

    for phase in range(SWEEPS + 1):
        halo_wait_sends(phase)
    spread_wait(count_in.at[peers], all_send.at[0])
    spread_wait(out_history.at[peers, row_part], all_send.at[1])
    spread_wait(out_state.at[peers, row_part], all_send.at[2])
    spread_wait(sum_in.at[peers], all_send.at[3])


def on_device(
    jump,
    external,
    cohesive,
    bond_mask,
    load_factor,
    arc_radius,
    stiffness,
    coupling,
    old_state,
    old_history,
    newton_steps,
    point_ids,
):
    nrow, ncol = lax.axis_size("row"), lax.axis_size("col")
    devices = nrow * ncol
    slots, cells = old_state.shape
    X, Y = cohesive.shape
    new_cap = slots // 2
    pair = 2 * ((slots + 2 * devices + 1) // (2 * devices))
    padded = 8 * ((pair + 7) // 8)
    phases = SWEEPS + 1
    vmem = pl.BlockSpec(memory_space=pltpu.VMEM)
    smem = pl.BlockSpec(memory_space=pltpu.SMEM)
    hbm = pl.BlockSpec(memory_space=pl.ANY)
    new_jump, new_load, new_state, new_history = pl.pallas_call(
        functools.partial(body, nrow, ncol, pair),
        out_shape=(
            jax.ShapeDtypeStruct(jump.shape, F32),
            jax.ShapeDtypeStruct((1, 1), F32),
            jax.ShapeDtypeStruct((new_cap, cells), F32),
            jax.ShapeDtypeStruct((new_cap, cells), F32),
        ),
        in_specs=[vmem] * 4 + [smem] * 2 + [vmem] * 3 + [hbm] * 3,
        out_specs=(vmem,) * 4,
        scratch_shapes=[
            pltpu.VMEM((cells, cells), BF16),
            pltpu.VMEM((slots, cells), F32),
            pltpu.VMEM((slots, cells), F32),
            pltpu.VMEM((slots, cells), F32),
            pltpu.VMEM((slots, cells), F32),
            pltpu.VMEM((2, slots, cells), BF16),
            pltpu.VMEM((1, cells), F32),
            pltpu.VMEM((8, LANES), F32),
            pltpu.VMEM((devices, 8, LANES), F32),
            pltpu.VMEM((8, Y), F32),
            pltpu.VMEM((devices, 8, Y), F32),
            pltpu.VMEM((phases, 2, 8, Y), F32),
            pltpu.VMEM((phases, 2, 8, Y), F32),
            pltpu.VMEM((phases, 2, X, Y), F32),
            pltpu.VMEM((phases, 2, X, Y), F32),
            pltpu.VMEM((devices, padded, cells), F32),
            pltpu.VMEM((devices, padded, cells), F32),
            pltpu.VMEM((devices, padded, cells), F32),
            pltpu.VMEM((devices, padded, cells), F32),
            pltpu.SemaphoreType.DMA((3,)),
            pltpu.SemaphoreType.DMA((phases, 4)),
            pltpu.SemaphoreType.DMA((phases, 4)),
            pltpu.SemaphoreType.DMA((4,)),
            pltpu.SemaphoreType.DMA((4,)),
        ],
        compiler_params=pltpu.CompilerParams(
            collective_id=0, has_side_effects=True, vmem_limit_bytes=60 * 1024 * 1024
        ),
    )(
        jump,
        external,
        cohesive,
        bond_mask,
        load_factor,
        arc_radius,
        coupling,
        newton_steps.reshape(1, slots),
        point_ids.reshape(1, slots),
        stiffness,
        old_state,
        old_history,
    )
    return new_jump, new_load.reshape(1), new_state, new_history


def solution(mesh):
    in_specs = (
        P(None, "row", "col"),
        P(None, "row", "col"),
        P("row", "col"),
        P(None, "row", "col"),
        P(),
        P(),
        P(),
        P(),
        P(("row", "col"), None),
        P(("row", "col"), None),
        P(("row", "col")),
        P(("row", "col")),
    )
    out_specs = (P(None, "row", "col"), P(), P(("row", "col"), None), P(("row", "col"), None))
    return jax.shard_map(
        on_device, mesh=mesh, in_specs=in_specs, out_specs=out_specs, check_vma=False
    )
```

time: 339 us -> 84.3 us (0.25)
  blocking collectives: 95.5 us -> 0 us
  Pallas kernels: 0 us -> 75 us
  local copies, waits for them, and re-layouts: 75.1 us -> 5.23 us
  starting transfers between devices: 59.2 us -> 0 us
  matrix products: 39.3 us -> 0 us
  other arithmetic: 31.1 us -> 0 us
  waiting for transfers between devices: 30.3 us -> 0 us
    pallas_call x0 -> x1, Pallas kernels: none -> 75 us  [on_device(): pl.pallas_call(functools.partial(body, nrow, ncol, pair), out_shape=(jax....]
    psum x1 -> x0, blocking collectives: 56.6 us -> none  [on_device(): lax.psum((jnp.sum(correction * direction), jnp.sum(direction * direction)...]
    ppermute x18 -> x0, starting transfers between devices: 47.5 us -> none  [the longest x8 28.7 us: extended(): lax.ppermute(tail, axis, [(i, (i + 1) % count) for i in range(ends)])]
    dot_general x12 -> x0, matrix products: 39.3 us -> none  [the longest x9 33.4 us: advance(): jnp.dot(current.astype(jnp.bfloat16), stiffness, preferred_element_type=j...]
    unnamed x1 -> x0, blocking collectives: 38.9 us -> none
    ppermute x18 -> x0, waiting for transfers between devices: 30.3 us -> none  [the longest x8 18.3 us: extended(): lax.ppermute(tail, axis, [(i, (i + 1) % count) for i in range(ends)])]
    gather x4 -> x0, local copies, waits for them, and re-layouts: 28.7 us -> none  [the longest x1 24.3 us: micro_solve(): diagonal = jnp.diagonal(stiffness).astype(jnp.float32)]
    slice x13 -> x0, local copies, waits for them, and re-layouts: 27 us -> none  [the longest x1 21.8 us: block_solve(): d00 = scale + tangent[0]]
  transfers between devices with their start and end apart: 20 -> 0, of which waited for: 8 -> 0; matrix products, arithmetic and copies ran while one was open for 40% -> 0% of each run, Pallas kernels for 0% -> 0%
where the time goes in v1:
time: 84.3 us; the launch traced here: 84 us
  Pallas kernels  75 us (89%)
  local copies, waits for them, and re-layouts  5.23 us (6%)
  between operations  3.7 us (4%)
    pallas_call x1, Pallas kernels, on_device(): pl.pallas_call(functools.partial(body, nrow, ncol, pair), out_shape=(jax....  75 us
    unnamed x3, local copies, waits for them, and re-layouts  5.23 us

profile of v1, /device:TPU:0, one launch (start us, length us, event | category | flops | bytes accessed | tf_op | source)
XLA Modules:
  0.0 84.0 jit_solution(11363167416693774092)
XLA Ops:
  1.9 75.0 %shard_map.147 = (f32[3,64,128]{2,1,0:T(8,128)}, f32[1,1]{1,0:T(1,128)}, f32[80,1536]{1,0:T(8,128)}, f32[80,1536]{1,0:T(8,128)}) custom-call(f32[3,64,128]{2,1,0:T(8,128)} %jump_ref.1, f32[3,64,128]{2,1,0:T(8,128)} %external_ref.1, f32[64,128]{1,0:T(8,128)} %cohesive_ref.1, s32[2,64,128]{2,1,0:T(8,128)} %bond_ref.1, f32[1]{0:T(128)S(6)} %copy.20.load_ref, ...), custom_call_target="tpu_custom_call" | custom-call | tf_op jit(solution)/shard_map/pallas_call | solution.py:469
  77.0 1.5 %copy.22 = f32[3,64,128]{2,1,0:T(8,128)} copy(f32[3,64,128]{2,1,0:T(8,128)} %get-tuple-element.16) | data formatting | bytes 196608
  79.1 1.8 %copy.24 = f32[80,1536]{1,0:T(8,128)} copy(f32[80,1536]{1,0:T(8,128)} %get-tuple-element.18) | data formatting | bytes 983040
  81.0 1.8 %copy.25 = f32[80,1536]{1,0:T(8,128)} copy(f32[80,1536]{1,0:T(8,128)} %get-tuple-element.19) | data formatting | bytes 983040
